TPU v7x, 32 devices: a whole 2x2x4 slice. The times are simulated.
32 devices in a mesh: tx: 4 (over x, core), ty: 4 (over z), src: 2 (over y).
Axes of the slice: x: 2, y: 2, z: 4, core: 2. Of those that a mesh axis runs over, the one named last changes fastest.
Arguments:
- spectrum: bfloat16 [2, 512, 512], P(None, ('tx', 'ty'), 'src'), may hold values from -0.0234375 to 0.0234375
- pupil_mask: int32 [256, 256], replicated, may hold values 0 or 1
- source_shifts: int32 [64, 2], P('src'), may hold values from 0 to 256
- source_weights: int32 [64], P('src'), may hold values from 0 to 8, as said below
Outputs:
- acid_level: float32 [2048, 1024], P(('tx', 'src'), 'ty')
Inputs may be any that keep to these rules, and one draw needn't show every extreme that they name: `source_weights`: the 32 consecutive sources of each group (one index of src) hold at least 4 points with weight above 0; some group has all 32 points on.
All inputs are finite; a program needn't handle non-finite values.
Results may differ from a plain program's by a relative error of at most 0.0017.
Values may be sent and summed in bfloat16 or wider, within the bound.
A program may use at most 64 MiB of HBM per device.

v0:
```python
import jax
import jax.numpy as jnp
from jax import lax
from jax.sharding import PartitionSpec as P

FRAME = 2048
BX = 512
BY = 256
diffusion_rate = 0.2
per_turn = 4


def padded_2(cells, sides, width):
    for axis, dim in sides:
        count = lax.axis_size(axis)
        ends = count - 1
        head = lax.slice_in_dim(cells, 0, width, axis=dim)
        tail = lax.slice_in_dim(cells, cells.shape[dim] - width, cells.shape[dim], axis=dim)
        cells = jnp.concatenate(
            [
                lax.ppermute(tail, axis, [(i, (i + 1) % count) for i in range(ends)]),
                cells,
                lax.ppermute(head, axis, [((i + 1) % count, i) for i in range(ends)]),
            ],
            axis=dim,
        )
    return cells


def phase_table(positions, frequency_count, frame_points):
    frequency = jnp.arange(frequency_count, dtype=jnp.int32) - frequency_count // 2
    phase_turns = positions[:, None] * frequency[None, :] % frame_points
    phase_angle = phase_turns.astype(jnp.float32) * (2.0 * jnp.pi / frame_points)
    return (jnp.cos(phase_angle), jnp.sin(phase_angle))


def rotation_table(cosine, sine):
    upper = jnp.concatenate([cosine, -sine], axis=1)
    lower = jnp.concatenate([sine, cosine], axis=1)
    return jnp.concatenate([upper, lower], axis=0).astype(jnp.bfloat16)


def diffuse(level, padded):
    beside = padded[2:, 1:-1] + padded[:-2, 1:-1] + padded[1:-1, 2:] + padded[1:-1, :-2]
    return level + diffusion_rate * (beside - 4.0 * level)


def arrange(shift_rows, weight_rows, slot_count, offset, stride):
    total_rows = weight_rows.shape[0]
    dead_flag = (weight_rows <= 0).astype(jnp.int32)
    live_order = jnp.argsort(dead_flag * total_rows + jnp.arange(total_rows, dtype=jnp.int32))
    live_count = jnp.sum(1 - dead_flag)
    pick_slots = offset + stride * jnp.arange(slot_count, dtype=jnp.int32)
    chosen = live_order[pick_slots]
    mine_count = jnp.maximum(live_count - offset + stride - 1, 0) // stride
    return (shift_rows[chosen], weight_rows[chosen], mine_count)


def windows(spectrum_all, pupil_bf, shift_batch, passband):

    def take_window(shift_pair):
        return lax.dynamic_slice(
            spectrum_all, (jnp.int32(0), shift_pair[0], shift_pair[1]), (2, passband, passband)
        )

    return jax.vmap(take_window)(shift_batch) * pupil_bf


def inner_block(window_cut, col_table):
    batch_count, _, passband, _ = window_cut.shape
    col_count = col_table.shape[1] // 2
    product = jnp.dot(
        window_cut.reshape(batch_count * 2 * passband, passband),
        col_table,
        preferred_element_type=jnp.float32,
    )
    product = product.reshape(batch_count, 2, passband, 2, col_count)
    real_part = product[:, 0, :, 0] - product[:, 1, :, 1]
    imag_part = product[:, 0, :, 1] + product[:, 1, :, 0]
    stacked = jnp.stack([real_part, imag_part], axis=0).astype(jnp.bfloat16)
    return stacked.transpose(0, 2, 1, 3).reshape(2 * passband, batch_count * col_count)


def power_sum(row_table, block_pair, weight_batch):
    row_total = row_table.shape[0] // 2
    batch_count = weight_batch.shape[0]
    field_pair = jnp.dot(row_table, block_pair, preferred_element_type=jnp.float32)
    square = field_pair[:row_total] ** 2 + field_pair[row_total:] ** 2
    square = square.reshape(row_total, batch_count, -1)
    return jnp.einsum("rbc,b->rc", square, weight_batch.astype(jnp.float32))


def owner_rows(row_count, passband):
    positions = lax.axis_index("tx") * BX + jnp.arange(row_count, dtype=jnp.int32)
    row_cos, row_sin = phase_table(positions, passband, FRAME)
    return rotation_table(row_cos, row_sin)


def body(spectrum, pupil_mask, source_shifts, source_weights):
    partial_spec = lax.all_gather(spectrum, "src", axis=2, tiled=True)
    spectrum_all = lax.all_gather(partial_spec, ("tx", "ty"), axis=1, tiled=True)
    passband = pupil_mask.shape[0]
    pupil_bf = pupil_mask.astype(jnp.bfloat16)
    group_count = lax.axis_size("src")
    slot_count = source_weights.shape[0]
    source_count = slot_count * group_count
    block_rows = BX // group_count
    all_shifts, all_weights = (
        lax.all_gather(source_shifts, "src", axis=0, tiled=True),
        lax.all_gather(source_weights, "src", axis=0, tiled=True),
    )
    chosen_shifts, chosen_weights, mine_count = arrange(
        all_shifts, all_weights, slot_count, lax.axis_index("src"), group_count
    )
    turn_count = (mine_count + per_turn - 1) // per_turn
    columns = lax.axis_index("ty") * BY + jnp.arange(BY, dtype=jnp.int32)
    col_cos, col_sin = phase_table(columns, passband, FRAME)
    col_table = jnp.concatenate([col_cos.T, col_sin.T], axis=1).astype(jnp.bfloat16)
    batch_shifts = chosen_shifts.reshape(slot_count // per_turn, per_turn, 2)
    batch_weights = chosen_weights.reshape(slot_count // per_turn, per_turn)

    def section_one(turn_index):
        return inner_block(
            windows(spectrum_all, pupil_bf, batch_shifts[turn_index], passband), col_table
        )

    row_table = owner_rows(BX, passband)

    def whole_turn(turn_index, running):
        return running + power_sum(row_table, section_one(turn_index), batch_weights[turn_index])

    partial_sum = lax.fori_loop(0, turn_count, whole_turn, jnp.zeros((BX, BY), jnp.float32))
    intensity_sum = lax.psum(partial_sum.astype(jnp.bfloat16), "src").astype(jnp.float32)
    acid_level = 1.0 - jnp.exp(-(intensity_sum / (2.0 * source_count)))
    for repeat in range(2):
        padded = padded_2(acid_level, (("tx", 0), ("ty", 1)), 1)
        acid_level = diffuse(acid_level, padded)
    acid_level = lax.dynamic_slice_in_dim(
        acid_level, lax.axis_index("src") * block_rows, block_rows, 0
    )
    return acid_level


def solution(mesh):
    placed = (P(None, ("tx", "ty"), "src"), P(), P("src", None), P("src"))
    return jax.shard_map(
        body, mesh=mesh, in_specs=placed, out_specs=P(("tx", "src"), "ty"), check_vma=False
    )
```

profile of v0, /device:TPU:0, one launch (start us, length us, event | category | flops | bytes accessed | tf_op | source)
XLA Modules:
  0.0 222.1 jit_solution(6561495545590390177)
XLA Ops:
  6.5 7.2 %all_gather.14 = bf16[2,32,512]{2,1,0:T(8,128)(2,1)} all-gather(bf16[2,32,256]{2,1,0:T(8,128)(2,1)} %param.6), channel_id=1, replica_groups=mesh['tx'=4,'ty'=4,'src'=2] {'src'}, dimensions={2}, use_global_device_ids=true | all-gather | bytes 98304 | tf_op jit(solution)/shard_map/all_gather | solution.py:100
  16.6 4.3 %all-reduce = s32[64]{0:T(128)S(1)} all-reduce(s32[64]{0:T(128)S(1)} %dynamic-update-slice.2), channel_id=1, replica_groups=mesh['tx'=4,'ty'=4,'src'=2] {'src'}, use_global_device_ids=true, to_apply=%add | all-reduce | flops 64 | bytes 512
  25.7 4.5 %all-gather = s32[2,32,2]{1,2,0:T(2,128)S(1)} all-gather(s32[1,32,2]{1,2,0:T(2,128)} %bitcast.113), channel_id=1, replica_groups=mesh['tx'=4,'ty'=4,'src'=2] {'src'}, dimensions={0}, use_global_device_ids=true | all-gather | bytes 768 | tf_op jit(solution)/shard_map/all_gather | solution.py:109
  33.3 2.5 %negate_convert_fusion = (bf16[512,256]{1,0:T(8,128)(2,1)S(1)}, bf16[512,256]{1,0:T(8,128)(2,1)S(1)}, bf16[512,256]{1,0:T(8,128)(2,1)S(1)}) fusion(s32[256]{0:T(256)S(1)} %get-tuple-element.148, s32[512]{0:T(512)S(1)} %iota_add_fusion), kind=kLoop, calls=%fused_computation.69 | loop fusion | flops 2359296 | bytes 789504 | tf_op jit(solution)/shard_map/convert.9
  36.9 15.4 %all-gather.3.cloned.1.call-done = bf16[2,512,512]{2,1,0:T(8,128)(2,1)} async-done(((bf16[2,32,512]{2,1,0:T(8,128)(2,1)}), bf16[2,512,512]{2,1,0:T(8,128)(2,1)}) %all-gather.3.cloned.1.call-update) | async-done | bytes 1048592 | tf_op jit(solution)/shard_map/all_gather | solution.py:101
  52.4 98.3 %while.13 = (s32[]{:T(128)}, f32[512,256]{1,0:T(8,128)S(1)}, s32[]{:T(128)}, s32[8,4,2]{1,2,0:T(2,128)S(1)}, bf16[2,512,512]{2,1,0:T(8,128)(2,1)}, /*index=5*/bf...) while((s32[]{:T(128)}, f32[512,256]{1,0:T(8,128)S(1)}, ...), condition=%wide.region_3.4_spmd, body=%wide.region_2.3_spmd.sunk | while | flops 1617559552 | bytes 34473136 | solution.py:132
  52.6 12.7 %while.14 = (s32[]{:T(128)}, bf16[2,512,512]{2,1,0:T(8,128)(2,1)}, s32[4,3]{1,0:T(4,128)S(1)}, bf16[4,2,256,256]{3,2,1,0:T(8,128)(2,1)S(1)}, s32[]{:T(128)}) while((s32[]{:T(128)}, bf16[2,512,512]{2,1,0:T(8,128)(2,1)}, s32[4,3]{1,0:T(4,128)S(1)}, bf16[4,2,256,256]{3,2,1,0:T(8,128)(2,1)S(1)}, s32[]{:T(128)}) %tuple.54), condition=%wide.while_cond, body=%wide.while_body.sunk | while | flops 2 | bytes 524413 | solution.py:62
  67.4 2.5 %convolution_bitcast_fusion.2 = f32[1024,1024]{0,1:T(8,128)S(1)} fusion(bf16[512,1024]{1,0:T(8,128)(2,1)S(1)} %bitcast.109, bf16[1024,512]{1,0:T(8,128)(2,1)} %get-tuple-element.298), kind=kOutput, calls=%fused_computation.5.clone.1 | convolution fusion | flops 1073741824 | bytes 6291456 | tf_op jit(solution)/shard_map/while/body/dot_general | solution.py:87
  72.2 12.7 %while.14 = (s32[]{:T(128)}, bf16[2,512,512]{2,1,0:T(8,128)(2,1)}, s32[4,3]{1,0:T(4,128)S(1)}, bf16[4,2,256,256]{3,2,1,0:T(8,128)(2,1)S(1)}, s32[]{:T(128)}) while((s32[]{:T(128)}, bf16[2,512,512]{2,1,0:T(8,128)(2,1)}, s32[4,3]{1,0:T(4,128)S(1)}, bf16[4,2,256,256]{3,2,1,0:T(8,128)(2,1)S(1)}, s32[]{:T(128)}) %tuple.54), condition=%wide.while_cond, body=%wide.while_body.sunk | while | flops 2 | bytes 524413 | solution.py:62
  87.1 2.5 %convolution_bitcast_fusion.2 = f32[1024,1024]{0,1:T(8,128)S(1)} fusion(bf16[512,1024]{1,0:T(8,128)(2,1)S(1)} %bitcast.109, bf16[1024,512]{1,0:T(8,128)(2,1)} %get-tuple-element.298), kind=kOutput, calls=%fused_computation.5.clone.1 | convolution fusion | flops 1073741824 | bytes 6291456 | tf_op jit(solution)/shard_map/while/body/dot_general | solution.py:87
  91.9 12.7 %while.14 = (s32[]{:T(128)}, bf16[2,512,512]{2,1,0:T(8,128)(2,1)}, s32[4,3]{1,0:T(4,128)S(1)}, bf16[4,2,256,256]{3,2,1,0:T(8,128)(2,1)S(1)}, s32[]{:T(128)}) while((s32[]{:T(128)}, bf16[2,512,512]{2,1,0:T(8,128)(2,1)}, s32[4,3]{1,0:T(4,128)S(1)}, bf16[4,2,256,256]{3,2,1,0:T(8,128)(2,1)S(1)}, s32[]{:T(128)}) %tuple.54), condition=%wide.while_cond, body=%wide.while_body.sunk | while | flops 2 | bytes 524413 | solution.py:62
  106.7 2.5 %convolution_bitcast_fusion.2 = f32[1024,1024]{0,1:T(8,128)S(1)} fusion(bf16[512,1024]{1,0:T(8,128)(2,1)S(1)} %bitcast.109, bf16[1024,512]{1,0:T(8,128)(2,1)} %get-tuple-element.298), kind=kOutput, calls=%fused_computation.5.clone.1 | convolution fusion | flops 1073741824 | bytes 6291456 | tf_op jit(solution)/shard_map/while/body/dot_general | solution.py:87
  111.5 12.7 %while.14 = (s32[]{:T(128)}, bf16[2,512,512]{2,1,0:T(8,128)(2,1)}, s32[4,3]{1,0:T(4,128)S(1)}, bf16[4,2,256,256]{3,2,1,0:T(8,128)(2,1)S(1)}, s32[]{:T(128)}) while((s32[]{:T(128)}, bf16[2,512,512]{2,1,0:T(8,128)(2,1)}, s32[4,3]{1,0:T(4,128)S(1)}, bf16[4,2,256,256]{3,2,1,0:T(8,128)(2,1)S(1)}, s32[]{:T(128)}) %tuple.54), condition=%wide.while_cond, body=%wide.while_body.sunk | while | flops 2 | bytes 524413 | solution.py:62
  126.4 2.5 %convolution_bitcast_fusion.2 = f32[1024,1024]{0,1:T(8,128)S(1)} fusion(bf16[512,1024]{1,0:T(8,128)(2,1)S(1)} %bitcast.109, bf16[1024,512]{1,0:T(8,128)(2,1)} %get-tuple-element.298), kind=kOutput, calls=%fused_computation.5.clone.1 | convolution fusion | flops 1073741824 | bytes 6291456 | tf_op jit(solution)/shard_map/while/body/dot_general | solution.py:87
  131.2 12.7 %while.14 = (s32[]{:T(128)}, bf16[2,512,512]{2,1,0:T(8,128)(2,1)}, s32[4,3]{1,0:T(4,128)S(1)}, bf16[4,2,256,256]{3,2,1,0:T(8,128)(2,1)S(1)}, s32[]{:T(128)}) while((s32[]{:T(128)}, bf16[2,512,512]{2,1,0:T(8,128)(2,1)}, s32[4,3]{1,0:T(4,128)S(1)}, bf16[4,2,256,256]{3,2,1,0:T(8,128)(2,1)S(1)}, s32[]{:T(128)}) %tuple.54), condition=%wide.while_cond, body=%wide.while_body.sunk | while | flops 2 | bytes 524413 | solution.py:62
  146.0 2.5 %convolution_bitcast_fusion.2 = f32[1024,1024]{0,1:T(8,128)S(1)} fusion(bf16[512,1024]{1,0:T(8,128)(2,1)S(1)} %bitcast.109, bf16[1024,512]{1,0:T(8,128)(2,1)} %get-tuple-element.298), kind=kOutput, calls=%fused_computation.5.clone.1 | convolution fusion | flops 1073741824 | bytes 6291456 | tf_op jit(solution)/shard_map/while/body/dot_general | solution.py:87
  151.4 22.4 %all-reduce.3.cloned.1.call-done = bf16[512,256]{1,0:T(8,128)(2,1)} async-done(((bf16[512,256]{1,0:T(8,128)(2,1)}), bf16[512,256]{1,0:T(8,128)(2,1)}) %all-reduce.3.cloned.1.call-update) | async-done | bytes 262160 | tf_op jit(solution)/shard_map/psum | solution.py:133
  177.5 3.5 %collective-permute-done = f32[1,256]{1,0:T(1,128)S(1)} collective-permute-done((f32[1,256]{1,0:T(1,128)S(1)}, f32[1,256]{1,0:T(1,128)S(1)}, u32[]{:S(2)}, u32[]{:S(2)}) %collective-permute-start) | collective-permute-done | bytes 1056 | tf_op jit(solution)/shard_map/ppermute | solution.py:23
  182.5 4.6 %collective-permute-start.3 = (f32[514,1]{1,0:T(8,128)S(1)}, f32[514,1]{1,0:T(8,128)S(1)}, u32[]{:S(2)}, u32[]{:S(2)}) collective-permute-start(f32[514,1]{1,0:T(8,128)S(1)} %get-tuple-element.136), channel_id=1, source_target_pairs={{0,2},{2,4},{4,6},{1,3},{3,5},{5,7},{8,10},{10,12},{12,14},{9,11},... | collective-permute-start | bytes 6176 | tf_op jit(solution)/shard_map/ppermute | solution.py:21
  187.0 3.9 %collective-permute-done.2 = f32[514,1]{1,0:T(8,128)S(1)} collective-permute-done((f32[514,1]{1,0:T(8,128)S(1)}, f32[514,1]{1,0:T(8,128)S(1)}, u32[]{:S(2)}, u32[]{:S(2)}) %collective-permute-start.2) | collective-permute-done | bytes 2088 | tf_op jit(solution)/shard_map/ppermute | solution.py:23
  193.2 3.1 %collective-permute-start.5 = (f32[1,256]{1,0:T(1,128)S(1)}, f32[1,256]{1,0:T(1,128)S(1)}, u32[]{:S(2)}, u32[]{:S(2)}) collective-permute-start(f32[1,256]{1,0:T(1,128)S(1)} %get-tuple-element.137), channel_id=1, source_target_pairs={{0,8},{8,16},{16,24},{1,9},{9,17},{17,25},{2,10},{10,18},{18,26},{... | collective-permute-start | bytes 3080 | tf_op jit(solution)/shard_map/ppermute | solution.py:21
  199.5 4.1 %collective-permute-start.7 = (f32[514,1]{1,0:T(8,128)S(1)}, f32[514,1]{1,0:T(8,128)S(1)}, u32[]{:S(2)}, u32[]{:S(2)}) collective-permute-start(f32[514,1]{1,0:T(8,128)S(1)} %get-tuple-element.133), channel_id=1, source_target_pairs={{0,2},{2,4},{4,6},{1,3},{3,5},{5,7},{8,10},{10,12},{12,14},{9,11},... | collective-permute-start | bytes 6176 | tf_op jit(solution)/shard_map/ppermute | solution.py:21
  205.2 4.4 %collective-permute-done.7 = f32[514,1]{1,0:T(8,128)S(1)} collective-permute-done((f32[514,1]{1,0:T(8,128)S(1)}, f32[514,1]{1,0:T(8,128)S(1)}, u32[]{:S(2)}, u32[]{:S(2)}) %collective-permute-start.7) | collective-permute-done | bytes 2088 | tf_op jit(solution)/shard_map/ppermute | solution.py:21
  209.5 4.7 %collective-permute-done.6 = f32[514,1]{1,0:T(8,128)S(1)} collective-permute-done((f32[514,1]{1,0:T(8,128)S(1)}, f32[514,1]{1,0:T(8,128)S(1)}, u32[]{:S(2)}, u32[]{:S(2)}) %collective-permute-start.6) | collective-permute-done | bytes 2088 | tf_op jit(solution)/shard_map/ppermute | solution.py:23
  (187 shorter events, 109.0 us)
Async XLA Ops:
  6.5 45.8 %all-gather.3.cloned.1.call-start = ((), (), s32[]{:S(2)}) async-start(), calls=%async_computation | async-start | bytes 1114112 | tf_op jit(solution)/shard_map/all_gather | solution.py:101
  13.8 160.1 %all-reduce.3.cloned.1.call-start = ((), (), s32[]{:S(2)}) async-start(), calls=%async_computation.1 | async-start | bytes 524288 | tf_op jit(solution)/shard_map/psum | solution.py:133
  174.9 2.6 %collective-permute-start.1 = (f32[1,256]{1,0:T(1,128)S(1)}, f32[1,256]{1,0:T(1,128)S(1)}, u32[]{:S(2)}, u32[]{:S(2)}) collective-permute-start(f32[1,256]{1,0:T(1,128)S(1)} %get-tuple-element.139), channel_id=1, source_target_pairs={{0,8},{8,16},{16,24},{1,9},{9,17},{17,25},{2,10},{10,18},{18,26},{... | collective-permute-start | bytes 3080 | tf_op jit(solution)/shard_map/ppermute | solution.py:21
  176.2 4.8 %collective-permute-start = (f32[1,256]{1,0:T(1,128)S(1)}, f32[1,256]{1,0:T(1,128)S(1)}, u32[]{:S(2)}, u32[]{:S(2)}) collective-permute-start(f32[1,256]{1,0:T(1,128)S(1)} %get-tuple-element.140), channel_id=1, source_target_pairs={{8,0},{16,8},{24,16},{9,1},{17,9},{25,17},{10,2},{18,10},{26,18},{... | collective-permute-start | bytes 3080 | tf_op jit(solution)/shard_map/ppermute | solution.py:23
  181.2 9.8 %collective-permute-start.2 = (f32[514,1]{1,0:T(8,128)S(1)}, f32[514,1]{1,0:T(8,128)S(1)}, u32[]{:S(2)}, u32[]{:S(2)}) collective-permute-start(f32[514,1]{1,0:T(8,128)S(1)} %get-tuple-element.135), channel_id=1, source_target_pairs={{2,0},{4,2},{6,4},{3,1},{5,3},{7,5},{10,8},{12,10},{14,12},{11,9},... | collective-permute-start | bytes 6176 | tf_op jit(solution)/shard_map/ppermute | solution.py:23
  182.5 10.2 %collective-permute-start.3 = (f32[514,1]{1,0:T(8,128)S(1)}, f32[514,1]{1,0:T(8,128)S(1)}, u32[]{:S(2)}, u32[]{:S(2)}) collective-permute-start(f32[514,1]{1,0:T(8,128)S(1)} %get-tuple-element.136), channel_id=1, source_target_pairs={{0,2},{2,4},{4,6},{1,3},{3,5},{5,7},{8,10},{10,12},{12,14},{9,11},... | collective-permute-start | bytes 6176 | tf_op jit(solution)/shard_map/ppermute | solution.py:21
  193.2 4.4 %collective-permute-start.5 = (f32[1,256]{1,0:T(1,128)S(1)}, f32[1,256]{1,0:T(1,128)S(1)}, u32[]{:S(2)}, u32[]{:S(2)}) collective-permute-start(f32[1,256]{1,0:T(1,128)S(1)} %get-tuple-element.137), channel_id=1, source_target_pairs={{0,8},{8,16},{16,24},{1,9},{9,17},{17,25},{2,10},{10,18},{18,26},{... | collective-permute-start | bytes 3080 | tf_op jit(solution)/shard_map/ppermute | solution.py:21
  196.3 3.1 %collective-permute-start.4 = (f32[1,256]{1,0:T(1,128)S(1)}, f32[1,256]{1,0:T(1,128)S(1)}, u32[]{:S(2)}, u32[]{:S(2)}) collective-permute-start(f32[1,256]{1,0:T(1,128)S(1)} %get-tuple-element.138), channel_id=1, source_target_pairs={{8,0},{16,8},{24,16},{9,1},{17,9},{25,17},{10,2},{18,10},{26,18},{... | collective-permute-start | bytes 3080 | tf_op jit(solution)/shard_map/ppermute | solution.py:23
  199.5 10.0 %collective-permute-start.7 = (f32[514,1]{1,0:T(8,128)S(1)}, f32[514,1]{1,0:T(8,128)S(1)}, u32[]{:S(2)}, u32[]{:S(2)}) collective-permute-start(f32[514,1]{1,0:T(8,128)S(1)} %get-tuple-element.133), channel_id=1, source_target_pairs={{0,2},{2,4},{4,6},{1,3},{3,5},{5,7},{8,10},{10,12},{12,14},{9,11},... | collective-permute-start | bytes 6176 | tf_op jit(solution)/shard_map/ppermute | solution.py:21
  203.7 10.6 %collective-permute-start.6 = (f32[514,1]{1,0:T(8,128)S(1)}, f32[514,1]{1,0:T(8,128)S(1)}, u32[]{:S(2)}, u32[]{:S(2)}) collective-permute-start(f32[514,1]{1,0:T(8,128)S(1)} %get-tuple-element.134), channel_id=1, source_target_pairs={{2,0},{4,2},{6,4},{3,1},{5,3},{7,5},{10,8},{12,10},{14,12},{11,9},... | collective-permute-start | bytes 6176 | tf_op jit(solution)/shard_map/ppermute | solution.py:23
Sparse Core Ops, SparseCore 0:
  13.9 38.4 all-gather.2
  151.6 22.2 all-reduce.2
where the time goes:
time: 224 us; the launch traced here: 222 us
  local copies, waits for them, and re-layouts  76.7 us (34%)
  waiting for transfers between devices  57.8 us (26%)
  matrix products  19.9 us (9%)
  starting transfers between devices  18.3 us (8%)
  other arithmetic  17.5 us (8%)
  blocking collectives  15.9 us (7%)
  between operations  14.9 us (7%)
    gather x60, local copies, waits for them, and re-layouts  62.8 us
    psum x1, waiting for transfers between devices, body(): lax.psum(partial_sum.astype(jnp.bfloat16), 'src').astype(jnp.float32)  22.4 us
    all_gather x1, waiting for transfers between devices, body(): lax.all_gather(partial_spec, ('tx', 'ty'), axis=1, tiled=True)  15.4 us
    ppermute x4, waiting for transfers between devices, padded_2(): lax.ppermute(head, axis, [((i + 1) % count, i) for i in range(ends)])  13.8 us
    ppermute x4, starting transfers between devices, padded_2(): lax.ppermute(tail, axis, [(i, (i + 1) % count) for i in range(ends)])  13.1 us
    dot_general x5, matrix products, power_sum(): jnp.dot(row_table, block_pair, preferred_element_type=jnp.float32)  12.7 us
    all_gather x1, blocking collectives, body(): partial_spec = lax.all_gather(spectrum, 'src', axis=2, tiled=True)  7.21 us
    ppermute x4, waiting for transfers between devices, padded_2(): lax.ppermute(tail, axis, [(i, (i + 1) % count) for i in range(ends)])  6.11 us
  transfers between devices with their start and end apart: 10, of which 8 were waited for; matrix products, arithmetic and copies ran while one was open for 6% of the time, Pallas kernels for 0%

commit v1 on v0

--- a/solution.py
+++ b/solution.py
@@ -98,7 +98,7 @@
 
 def body(spectrum, pupil_mask, source_shifts, source_weights):
     partial_spec = lax.all_gather(spectrum, "src", axis=2, tiled=True)
-    spectrum_all = lax.all_gather(partial_spec, ("tx", "ty"), axis=1, tiled=True)
+    spectrum_all = jnp.concatenate(lax.all_gather(partial_spec, ("tx", "ty")), axis=1)
     passband = pupil_mask.shape[0]
     pupil_bf = pupil_mask.astype(jnp.bfloat16)
     group_count = lax.axis_size("src")

time: 224 us -> 210 us (0.938)
  local copies, waits for them, and re-layouts: 76.7 us -> 62.8 us
    gather x60, local copies, waits for them, and re-layouts: 62.8 us -> 41 us
    while x10 -> x30, local copies, waits for them, and re-layouts: 1.55 us -> 7.29 us
where the time goes in v1:
time: 210 us; the launch traced here: 209 us
  local copies, waits for them, and re-layouts  62.8 us (30%)
  waiting for transfers between devices  57.7 us (27%)
  matrix products  19.9 us (9%)
  other arithmetic  18.6 us (9%)
  starting transfers between devices  18.3 us (9%)
  blocking collectives  15.9 us (8%)
  between operations  14.9 us (7%)
    gather x60, local copies, waits for them, and re-layouts  41 us
    psum x1, waiting for transfers between devices, body(): lax.psum(partial_sum.astype(jnp.bfloat16), 'src').astype(jnp.float32)  22.4 us
    all_gather x1, waiting for transfers between devices, body(): lax.all_gather(partial_spec, ('tx', 'ty'))  15.3 us
    ppermute x4, waiting for transfers between devices, padded_2(): lax.ppermute(head, axis, [((i + 1) % count, i) for i in range(ends)])  13.8 us
    ppermute x4, starting transfers between devices, padded_2(): lax.ppermute(tail, axis, [(i, (i + 1) % count) for i in range(ends)])  13.1 us
    dot_general x5, matrix products, power_sum(): jnp.dot(row_table, block_pair, preferred_element_type=jnp.float32)  12.7 us
    while x30, local copies, waits for them, and re-layouts  7.29 us
    all_gather x1, blocking collectives, body(): partial_spec = lax.all_gather(spectrum, 'src', axis=2, tiled=True)  7.21 us
  transfers between devices with their start and end apart: 10, of which 8 were waited for; matrix products, arithmetic and copies ran while one was open for 6% of the time, Pallas kernels for 0%

profile of v1, /device:TPU:0, one launch (start us, length us, event | category | flops | bytes accessed | tf_op | source)
XLA Modules:
  0.0 208.9 jit_solution(5202381645745692257)
XLA Ops:
  6.5 7.2 %all_gather.17 = bf16[2,32,512]{2,1,0:T(8,128)(2,1)} all-gather(bf16[2,32,256]{2,1,0:T(8,128)(2,1)} %param.6), channel_id=1, replica_groups=mesh['tx'=4,'ty'=4,'src'=2] {'src'}, dimensions={2}, use_global_device_ids=true | all-gather | bytes 98304 | tf_op jit(solution)/shard_map/all_gather | solution.py:100
  16.6 4.3 %all-reduce = s32[64]{0:T(128)S(1)} all-reduce(s32[64]{0:T(128)S(1)} %dynamic-update-slice.2), channel_id=1, replica_groups=mesh['tx'=4,'ty'=4,'src'=2] {'src'}, use_global_device_ids=true, to_apply=%add | all-reduce | flops 64 | bytes 512
  25.9 4.5 %all-gather.1 = s32[2,32,2]{1,2,0:T(2,128)S(1)} all-gather(s32[1,32,2]{1,2,0:T(2,128)} %bitcast.119), channel_id=1, replica_groups=mesh['tx'=4,'ty'=4,'src'=2] {'src'}, dimensions={0}, use_global_device_ids=true | all-gather | bytes 768 | tf_op jit(solution)/shard_map/all_gather | solution.py:109
  33.4 2.5 %negate_convert_fusion = (bf16[512,256]{1,0:T(8,128)(2,1)S(1)}, bf16[512,256]{1,0:T(8,128)(2,1)S(1)}, bf16[512,256]{1,0:T(8,128)(2,1)S(1)}) fusion(s32[256]{0:T(256)S(1)} %get-tuple-element.148, s32[512]{0:T(512)S(1)} %iota_add_fusion), kind=kLoop, calls=%fused_computation.69 | loop fusion | flops 2359296 | bytes 789504 | tf_op jit(solution)/shard_map/convert.9
  37.0 15.3 %all-gather.4.cloned.1.call-done = bf16[32,32,512]{2,1,0:T(8,128)(2,1)} async-done(((bf16[2,32,512]{2,1,0:T(8,128)(2,1)}), bf16[32,32,512]{2,1,0:T(8,128)(2,1)}) %all-gather.4.cloned.1.call-update) | async-done | bytes 1048592 | tf_op jit(solution)/shard_map/all_gather | solution.py:101
  54.4 82.0 %while.13 = (s32[]{:T(128)}, f32[512,256]{1,0:T(8,128)}, s32[]{:T(128)}, s32[8,4,2]{1,2,0:T(2,128)S(1)}, bf16[2,512,512]{2,1,0:T(8,128)(2,1)S(1)}, /*index=5*/bf...) while((s32[]{:T(128)}, f32[512,256]{1,0:T(8,128)}, ...), condition=%wide.region_3.4_spmd, body=%wide.region_2.3_spmd.sunk | while | flops 1617559552 | bytes 38667496 | solution.py:132
  54.6 8.3 %while.14 = (s32[]{:T(128)}, bf16[2,512,512]{2,1,0:T(8,128)(2,1)S(1)}, s32[4,3]{1,0:T(4,128)S(1)}, bf16[4,2,256,256]{3,2,1,0:T(8,128)(2,1)S(1)}, s32[]{:T(128)}) while((s32[]{:T(128)}, bf16[2,512,512]{2,1,0:T(8,128)(2,1)S(1)}, s32[4,3]{1,0:T(4,128)S(1)}, bf16[4,2,256,256]{3,2,1,0:T(8,128)(2,1)S(1)}, s32[]{:T(128)}) %tuple.54), condition=%wide.while_cond, body=%wide.while_body.sunk | while | flops 2 | bytes 524413 | solution.py:62
  65.0 2.5 %convolution_bitcast_fusion.2 = f32[1024,1024]{0,1:T(8,128)S(1)} fusion(bf16[512,1024]{1,0:T(8,128)(2,1)S(1)} %bitcast.114, bf16[1024,512]{1,0:T(8,128)(2,1)} %get-tuple-element.298), kind=kOutput, calls=%fused_computation.5.clone.1 | convolution fusion | flops 1073741824 | bytes 6291456 | tf_op jit(solution)/shard_map/while/body/dot_general | solution.py:87
  71.0 8.3 %while.14 = (s32[]{:T(128)}, bf16[2,512,512]{2,1,0:T(8,128)(2,1)S(1)}, s32[4,3]{1,0:T(4,128)S(1)}, bf16[4,2,256,256]{3,2,1,0:T(8,128)(2,1)S(1)}, s32[]{:T(128)}) while((s32[]{:T(128)}, bf16[2,512,512]{2,1,0:T(8,128)(2,1)S(1)}, s32[4,3]{1,0:T(4,128)S(1)}, bf16[4,2,256,256]{3,2,1,0:T(8,128)(2,1)S(1)}, s32[]{:T(128)}) %tuple.54), condition=%wide.while_cond, body=%wide.while_body.sunk | while | flops 2 | bytes 524413 | solution.py:62
  81.4 2.5 %convolution_bitcast_fusion.2 = f32[1024,1024]{0,1:T(8,128)S(1)} fusion(bf16[512,1024]{1,0:T(8,128)(2,1)S(1)} %bitcast.114, bf16[1024,512]{1,0:T(8,128)(2,1)} %get-tuple-element.298), kind=kOutput, calls=%fused_computation.5.clone.1 | convolution fusion | flops 1073741824 | bytes 6291456 | tf_op jit(solution)/shard_map/while/body/dot_general | solution.py:87
  87.4 8.3 %while.14 = (s32[]{:T(128)}, bf16[2,512,512]{2,1,0:T(8,128)(2,1)S(1)}, s32[4,3]{1,0:T(4,128)S(1)}, bf16[4,2,256,256]{3,2,1,0:T(8,128)(2,1)S(1)}, s32[]{:T(128)}) while((s32[]{:T(128)}, bf16[2,512,512]{2,1,0:T(8,128)(2,1)S(1)}, s32[4,3]{1,0:T(4,128)S(1)}, bf16[4,2,256,256]{3,2,1,0:T(8,128)(2,1)S(1)}, s32[]{:T(128)}) %tuple.54), condition=%wide.while_cond, body=%wide.while_body.sunk | while | flops 2 | bytes 524413 | solution.py:62
  97.8 2.5 %convolution_bitcast_fusion.2 = f32[1024,1024]{0,1:T(8,128)S(1)} fusion(bf16[512,1024]{1,0:T(8,128)(2,1)S(1)} %bitcast.114, bf16[1024,512]{1,0:T(8,128)(2,1)} %get-tuple-element.298), kind=kOutput, calls=%fused_computation.5.clone.1 | convolution fusion | flops 1073741824 | bytes 6291456 | tf_op jit(solution)/shard_map/while/body/dot_general | solution.py:87
  103.8 8.3 %while.14 = (s32[]{:T(128)}, bf16[2,512,512]{2,1,0:T(8,128)(2,1)S(1)}, s32[4,3]{1,0:T(4,128)S(1)}, bf16[4,2,256,256]{3,2,1,0:T(8,128)(2,1)S(1)}, s32[]{:T(128)}) while((s32[]{:T(128)}, bf16[2,512,512]{2,1,0:T(8,128)(2,1)S(1)}, s32[4,3]{1,0:T(4,128)S(1)}, bf16[4,2,256,256]{3,2,1,0:T(8,128)(2,1)S(1)}, s32[]{:T(128)}) %tuple.54), condition=%wide.while_cond, body=%wide.while_body.sunk | while | flops 2 | bytes 524413 | solution.py:62
  114.2 2.5 %convolution_bitcast_fusion.2 = f32[1024,1024]{0,1:T(8,128)S(1)} fusion(bf16[512,1024]{1,0:T(8,128)(2,1)S(1)} %bitcast.114, bf16[1024,512]{1,0:T(8,128)(2,1)} %get-tuple-element.298), kind=kOutput, calls=%fused_computation.5.clone.1 | convolution fusion | flops 1073741824 | bytes 6291456 | tf_op jit(solution)/shard_map/while/body/dot_general | solution.py:87
  120.2 8.3 %while.14 = (s32[]{:T(128)}, bf16[2,512,512]{2,1,0:T(8,128)(2,1)S(1)}, s32[4,3]{1,0:T(4,128)S(1)}, bf16[4,2,256,256]{3,2,1,0:T(8,128)(2,1)S(1)}, s32[]{:T(128)}) while((s32[]{:T(128)}, bf16[2,512,512]{2,1,0:T(8,128)(2,1)S(1)}, s32[4,3]{1,0:T(4,128)S(1)}, bf16[4,2,256,256]{3,2,1,0:T(8,128)(2,1)S(1)}, s32[]{:T(128)}) %tuple.54), condition=%wide.while_cond, body=%wide.while_body.sunk | while | flops 2 | bytes 524413 | solution.py:62
  130.6 2.5 %convolution_bitcast_fusion.2 = f32[1024,1024]{0,1:T(8,128)S(1)} fusion(bf16[512,1024]{1,0:T(8,128)(2,1)S(1)} %bitcast.114, bf16[1024,512]{1,0:T(8,128)(2,1)} %get-tuple-element.298), kind=kOutput, calls=%fused_computation.5.clone.1 | convolution fusion | flops 1073741824 | bytes 6291456 | tf_op jit(solution)/shard_map/while/body/dot_general | solution.py:87
  138.2 22.4 %all-reduce.3.cloned.1.call-done = bf16[512,256]{1,0:T(8,128)(2,1)} async-done(((bf16[512,256]{1,0:T(8,128)(2,1)}), bf16[512,256]{1,0:T(8,128)(2,1)}) %all-reduce.3.cloned.1.call-update) | async-done | bytes 262160 | tf_op jit(solution)/shard_map/psum | solution.py:133
  164.3 3.4 %collective-permute-done = f32[1,256]{1,0:T(1,128)S(1)} collective-permute-done((f32[1,256]{1,0:T(1,128)S(1)}, f32[1,256]{1,0:T(1,128)S(1)}, u32[]{:S(2)}, u32[]{:S(2)}) %collective-permute-start) | collective-permute-done | bytes 1056 | tf_op jit(solution)/shard_map/ppermute | solution.py:23
  169.3 4.6 %collective-permute-start.3 = (f32[514,1]{1,0:T(8,128)S(1)}, f32[514,1]{1,0:T(8,128)S(1)}, u32[]{:S(2)}, u32[]{:S(2)}) collective-permute-start(f32[514,1]{1,0:T(8,128)S(1)} %get-tuple-element.136), channel_id=1, source_target_pairs={{0,2},{2,4},{4,6},{1,3},{3,5},{5,7},{8,10},{10,12},{12,14},{9,11},... | collective-permute-start | bytes 6176 | tf_op jit(solution)/shard_map/ppermute | solution.py:21
  173.8 3.9 %collective-permute-done.2 = f32[514,1]{1,0:T(8,128)S(1)} collective-permute-done((f32[514,1]{1,0:T(8,128)S(1)}, f32[514,1]{1,0:T(8,128)S(1)}, u32[]{:S(2)}, u32[]{:S(2)}) %collective-permute-start.2) | collective-permute-done | bytes 2088 | tf_op jit(solution)/shard_map/ppermute | solution.py:23
  180.0 3.1 %collective-permute-start.5 = (f32[1,256]{1,0:T(1,128)S(1)}, f32[1,256]{1,0:T(1,128)S(1)}, u32[]{:S(2)}, u32[]{:S(2)}) collective-permute-start(f32[1,256]{1,0:T(1,128)S(1)} %get-tuple-element.137), channel_id=1, source_target_pairs={{0,8},{8,16},{16,24},{1,9},{9,17},{17,25},{2,10},{10,18},{18,26},{... | collective-permute-start | bytes 3080 | tf_op jit(solution)/shard_map/ppermute | solution.py:21
  186.3 4.1 %collective-permute-start.7 = (f32[514,1]{1,0:T(8,128)S(1)}, f32[514,1]{1,0:T(8,128)S(1)}, u32[]{:S(2)}, u32[]{:S(2)}) collective-permute-start(f32[514,1]{1,0:T(8,128)S(1)} %get-tuple-element.133), channel_id=1, source_target_pairs={{0,2},{2,4},{4,6},{1,3},{3,5},{5,7},{8,10},{10,12},{12,14},{9,11},... | collective-permute-start | bytes 6176 | tf_op jit(solution)/shard_map/ppermute | solution.py:21
  191.9 4.4 %collective-permute-done.7 = f32[514,1]{1,0:T(8,128)S(1)} collective-permute-done((f32[514,1]{1,0:T(8,128)S(1)}, f32[514,1]{1,0:T(8,128)S(1)}, u32[]{:S(2)}, u32[]{:S(2)}) %collective-permute-start.7) | collective-permute-done | bytes 2088 | tf_op jit(solution)/shard_map/ppermute | solution.py:21
  196.3 4.7 %collective-permute-done.6 = f32[514,1]{1,0:T(8,128)S(1)} collective-permute-done((f32[514,1]{1,0:T(8,128)S(1)}, f32[514,1]{1,0:T(8,128)S(1)}, u32[]{:S(2)}, u32[]{:S(2)}) %collective-permute-start.6) | collective-permute-done | bytes 2088 | tf_op jit(solution)/shard_map/ppermute | solution.py:23
  (208 shorter events, 96.0 us)
Async XLA Ops:
  6.5 45.8 %all-gather.4.cloned.1.call-start = ((), (), s32[]{:S(2)}) async-start(), calls=%async_computation.1 | async-start | bytes 1114112 | tf_op jit(solution)/shard_map/all_gather | solution.py:101
  13.8 146.9 %all-reduce.3.cloned.1.call-start = ((), (), s32[]{:S(2)}) async-start(), calls=%async_computation | async-start | bytes 524288 | tf_op jit(solution)/shard_map/psum | solution.py:133
  68.9 1.0 copy-start
  70.0 0.8 copy-start.1
  85.3 1.0 copy-start
  86.4 0.8 copy-start.1
  101.7 1.0 copy-start
  102.8 0.8 copy-start.1
  118.1 1.0 copy-start
  119.2 0.8 copy-start.1
  134.5 1.0 copy-start
  135.6 0.8 copy-start.1
  161.7 2.6 %collective-permute-start.1 = (f32[1,256]{1,0:T(1,128)S(1)}, f32[1,256]{1,0:T(1,128)S(1)}, u32[]{:S(2)}, u32[]{:S(2)}) collective-permute-start(f32[1,256]{1,0:T(1,128)S(1)} %get-tuple-element.139), channel_id=1, source_target_pairs={{0,8},{8,16},{16,24},{1,9},{9,17},{17,25},{2,10},{10,18},{18,26},{... | collective-permute-start | bytes 3080 | tf_op jit(solution)/shard_map/ppermute | solution.py:21
  163.0 4.8 %collective-permute-start = (f32[1,256]{1,0:T(1,128)S(1)}, f32[1,256]{1,0:T(1,128)S(1)}, u32[]{:S(2)}, u32[]{:S(2)}) collective-permute-start(f32[1,256]{1,0:T(1,128)S(1)} %get-tuple-element.140), channel_id=1, source_target_pairs={{8,0},{16,8},{24,16},{9,1},{17,9},{25,17},{10,2},{18,10},{26,18},{... | collective-permute-start | bytes 3080 | tf_op jit(solution)/shard_map/ppermute | solution.py:23
  168.0 9.8 %collective-permute-start.2 = (f32[514,1]{1,0:T(8,128)S(1)}, f32[514,1]{1,0:T(8,128)S(1)}, u32[]{:S(2)}, u32[]{:S(2)}) collective-permute-start(f32[514,1]{1,0:T(8,128)S(1)} %get-tuple-element.135), channel_id=1, source_target_pairs={{2,0},{4,2},{6,4},{3,1},{5,3},{7,5},{10,8},{12,10},{14,12},{11,9},... | collective-permute-start | bytes 6176 | tf_op jit(solution)/shard_map/ppermute | solution.py:23
  169.3 10.2 %collective-permute-start.3 = (f32[514,1]{1,0:T(8,128)S(1)}, f32[514,1]{1,0:T(8,128)S(1)}, u32[]{:S(2)}, u32[]{:S(2)}) collective-permute-start(f32[514,1]{1,0:T(8,128)S(1)} %get-tuple-element.136), channel_id=1, source_target_pairs={{0,2},{2,4},{4,6},{1,3},{3,5},{5,7},{8,10},{10,12},{12,14},{9,11},... | collective-permute-start | bytes 6176 | tf_op jit(solution)/shard_map/ppermute | solution.py:21
  180.0 4.4 %collective-permute-start.5 = (f32[1,256]{1,0:T(1,128)S(1)}, f32[1,256]{1,0:T(1,128)S(1)}, u32[]{:S(2)}, u32[]{:S(2)}) collective-permute-start(f32[1,256]{1,0:T(1,128)S(1)} %get-tuple-element.137), channel_id=1, source_target_pairs={{0,8},{8,16},{16,24},{1,9},{9,17},{17,25},{2,10},{10,18},{18,26},{... | collective-permute-start | bytes 3080 | tf_op jit(solution)/shard_map/ppermute | solution.py:21
  183.1 3.1 %collective-permute-start.4 = (f32[1,256]{1,0:T(1,128)S(1)}, f32[1,256]{1,0:T(1,128)S(1)}, u32[]{:S(2)}, u32[]{:S(2)}) collective-permute-start(f32[1,256]{1,0:T(1,128)S(1)} %get-tuple-element.138), channel_id=1, source_target_pairs={{8,0},{16,8},{24,16},{9,1},{17,9},{25,17},{10,2},{18,10},{26,18},{... | collective-permute-start | bytes 3080 | tf_op jit(solution)/shard_map/ppermute | solution.py:23
  186.3 10.0 %collective-permute-start.7 = (f32[514,1]{1,0:T(8,128)S(1)}, f32[514,1]{1,0:T(8,128)S(1)}, u32[]{:S(2)}, u32[]{:S(2)}) collective-permute-start(f32[514,1]{1,0:T(8,128)S(1)} %get-tuple-element.133), channel_id=1, source_target_pairs={{0,2},{2,4},{4,6},{1,3},{3,5},{5,7},{8,10},{10,12},{12,14},{9,11},... | collective-permute-start | bytes 6176 | tf_op jit(solution)/shard_map/ppermute | solution.py:21
  190.4 10.6 %collective-permute-start.6 = (f32[514,1]{1,0:T(8,128)S(1)}, f32[514,1]{1,0:T(8,128)S(1)}, u32[]{:S(2)}, u32[]{:S(2)}) collective-permute-start(f32[514,1]{1,0:T(8,128)S(1)} %get-tuple-element.134), channel_id=1, source_target_pairs={{2,0},{4,2},{6,4},{3,1},{5,3},{7,5},{10,8},{12,10},{14,12},{11,9},... | collective-permute-start | bytes 6176 | tf_op jit(solution)/shard_map/ppermute | solution.py:23
Sparse Core Ops, SparseCore 0:
  13.9 38.3 all-gather.3
  138.4 22.2 all-reduce.2
